TPU v7x, 32 devices: a whole 2x2x4 slice. The times are simulated.
32 devices in a mesh: gx: 4 (over y, core), gy: 2 (over x), gz: 4 (over z).
Axes of the slice: x: 2, y: 2, z: 4, core: 2. Of those that a mesh axis runs over, the one named last changes fastest.
Arguments:
- density: float32 [32, 32, 512], P('gx', 'gy', 'gz'), may hold values from 0.7 to 1.6
- momentum: float32 [32, 32, 512], P('gx', 'gy', 'gz'), may hold values from -7 to 7
- hydrogen: float32 [32, 32, 512], P('gx', 'gy', 'gz'), may hold values from 0.05 to 1.2
- forced_modes: int32 [96, 3], replicated, may hold values from -3 to 3, as said below
Outputs:
- density_rate: float32 [32, 32, 512], P('gx', 'gy', 'gz')
- momentum_rate: float32 [32, 32, 512], P('gx', 'gy', 'gz')
- hydrogen_rate: float32 [32, 32, 512], P('gx', 'gy', 'gz')
Inputs may be any that keep to these rules, and one draw needn't show every extreme that they name: `forced_modes`: each row is a wave vector (kx, ky, kz) with 1 <= kx^2 + ky^2 + kz^2 <= 9; the 96 rows are distinct.
All inputs are finite; a program needn't handle non-finite values.
Results may differ from a plain program's by a relative error of at most 0.0003.
Values sent between devices are 32-bit elements; how exact they have to be, the bound alone decides.
No kernel may reach another device: no remote copies, remote signals or barrier semaphores. Data moves between devices by JAX's collectives and lax.ppermute only.
A program may use at most 64 MiB of HBM per device.

v0:
```python
import functools
import math

import jax
import jax.numpy as jnp
import numpy as np
from jax import lax
from jax.experimental import pallas as pl
from jax.experimental.pallas import tpu as pltpu
from jax.sharding import PartitionSpec as P


KMAX = 3
HALO = 4
AXES = ("gx", "gy", "gz")

FIRST_COEFFS = (0.8, -0.2, 4.0 / 105.0, -1.0 / 280.0)
SECOND_COEFFS = (1.6, -0.2, 8.0 / 315.0, -1.0 / 560.0)
CENTRE_COEFF = -205.0 / 72.0
VISCOSITY = 0.3
DIFFUSIVITY = 1.5
FORCE_POWER = 0.3
ENERGY_EPS = 1e-06
ACTIVATION = 2.0
HIGHEST = lax.Precision.HIGHEST

HALF_PLANE = [(0, ky) for ky in range(KMAX + 1)] + [
    (kx, ky) for kx in range(1, KMAX + 1) for ky in range(-KMAX, KMAX + 1)
]


def plane_table(local_x, local_y, full_x, full_y):
    x = np.arange(local_x)[:, None]
    y = np.arange(local_y)[None, :]
    table = np.zeros((local_x * local_y, 128), np.float64)
    for lane, (kx, ky) in enumerate(HALF_PLANE):
        angle = 2.0 * np.pi * (kx * x / full_x + ky * y / full_y)
        table[:, lane] = np.cos(angle).reshape(-1)
        table[:, 32 + lane] = np.sin(angle).reshape(-1)
    return table.astype(np.float32)


def line_table(local_z, full_z):
    z = np.arange(local_z)
    table = np.zeros((8, local_z), np.float64)
    for kz in range(KMAX + 1):
        angle = 2.0 * np.pi * kz * z / full_z
        table[kz] = np.cos(angle)
        table[4 + kz] = np.sin(angle)
    return table.astype(np.float32)


def rotation_tables(counts):
    count_x, count_y, count_z = counts
    lane = np.arange(128)
    wave = lane % 32
    kx = np.array([HALF_PLANE[w][0] if w < len(HALF_PLANE) else 0 for w in wave])
    ky = np.array([HALF_PLANE[w][1] if w < len(HALF_PLANE) else 0 for w in wave])
    sign_xy = np.where(lane & 32, 1.0, -1.0)
    sign_z = np.where(lane & 64, 1.0, -1.0)
    plane = np.zeros((count_x, count_y, 2, 4, 128))
    for i in range(count_x):
        for j in range(count_y):
            angle = 2.0 * np.pi * ((kx * i % count_x) / count_x + (ky * j % count_y) / count_y)
            plane[i, j, 0] = np.cos(angle)
            plane[i, j, 1] = np.sin(angle) * sign_xy
    line = np.zeros((count_z, 2, 4, 128))
    for k in range(count_z):
        angle = 2.0 * np.pi * ((np.arange(4) * k) % count_z) / count_z
        line[k, 0] = np.cos(angle)[:, None]
        line[k, 1] = np.sin(angle)[:, None] * sign_z[None, :]
    plane = plane.reshape(count_x * count_y, 2, 4, 128)
    return plane.astype(np.float32), line.astype(np.float32)


def lanes_of(shape):
    return lax.broadcasted_iota(jnp.int32, shape, len(shape) - 1)


def swap32(a):
    bit = (lanes_of(a.shape) & 32) != 0
    return jnp.where(bit, pltpu.roll(a, 32, 1), pltpu.roll(a, 96, 1))


def swap64(a):
    return pltpu.roll(a, 64, 1)


def fetch_all(sources, targets, sems):
    copies = [pltpu.make_async_copy(a, b, sems.at[n])
              for n, (a, b) in enumerate(zip(sources, targets))]
    for copy in copies:
        copy.start()
    return copies


def rotations(plane_ref, line_ref):
    place = lax.axis_index("gx") * lax.axis_size("gy") + lax.axis_index("gy")
    level = lax.axis_index("gz")
    return plane_ref[place, 0], plane_ref[place, 1], line_ref[level, 0], line_ref[level, 1]


def pre_kernel(slots, *refs):
    sources, targets = refs[:8], refs[8:16]
    part_out, low_ref, high_ref, side_ref, depth_ref, part_ref, sems, part_sem = refs[16:]
    copies = fetch_all(sources, targets, sems)
    d_ref, m_ref, plane_ref, line_ref, rot_plane_ref, rot_line_ref, h_ref, _ = targets
    size_x, size_y, size_z = d_ref.shape
    for copy in copies[:6]:
        copy.wait()
    rot = rotations(rot_plane_ref, rot_line_ref)
    flat = (m_ref[...] / d_ref[...]).reshape(size_x * size_y, size_z)
    along = lax.dot_general(line_ref[...], flat, (((1,), (1,)), ((), ())), precision=HIGHEST,
                            preferred_element_type=jnp.float32)
    both = jnp.dot(along, plane_ref[...], precision=HIGHEST, preferred_element_type=jnp.float32)
    part = both[0:4] + swap64(both)[4:8]
    part = rot[0] * part + rot[1] * swap32(part)
    part = rot[2] * part + rot[3] * swap64(part)
    part_ref[...] = jnp.broadcast_to(part[None], (slots, 4, 128))
    send = pltpu.make_async_copy(part_ref, part_out, part_sem)
    send.start()
    for copy in copies[6:]:
        copy.wait()
    for index, ref in enumerate((d_ref, m_ref, h_ref)):
        low_ref[index] = ref[0:HALO]
        high_ref[index] = ref[size_x - HALO:size_x]
    lane = lanes_of((size_y, size_z))
    depth = jnp.zeros((size_y, 128), jnp.float32)
    for f, ref in enumerate((m_ref, h_ref)):
        for i in range(size_x):
            plane = ref[i]
            side_ref[f, i, 0:HALO] = plane[0:HALO]
            side_ref[f, i, HALO:] = plane[size_y - HALO:]
            at = 2 * HALO * (f * size_x + i)
            first = pltpu.roll(plane, at, 1)
            last = pltpu.roll(plane, (at + 2 * HALO) % size_z, 1)
            depth = jnp.where((lane >= at) & (lane < at + HALO), first, depth)
            depth = jnp.where((lane >= at + HALO) & (lane < at + 2 * HALO), last, depth)
    depth_ref[...] = depth
    send.wait()


def mode_counts(modes):
    kx, ky, kz = modes[0:1], modes[1:2], modes[2:3]
    flip = jnp.where((kx < 0) | ((kx == 0) & (ky < 0)), -1, 1)
    kx, ky, kz = kx * flip, ky * flip, kz * flip
    width = 2 * KMAX + 1
    wave = jnp.where(kx == 0, ky, KMAX + 1 + (kx - 1) * width + ky + KMAX)
    code = wave + jnp.where(kz < 0, 64, 0)
    count = modes.shape[1]
    row = lax.broadcasted_iota(jnp.int32, (128, count), 0)
    hit = jnp.where((row & 95) == code, 1.0, 0.0)
    level = jnp.where(lax.broadcasted_iota(jnp.int32, (8, count), 0) == jnp.abs(kz), 1.0, 0.0)
    counts = lax.dot_general(level, hit, (((1,), (1,)), ((), ())),
                             preferred_element_type=jnp.float32)
    return counts[0:4]


def local_kernel(d_ref, m_ref, h_ref, modes_ref, density_ref, momentum_ref, hydrogen_ref,
                 weight_ref, pad_ref):
    size_x, size_y, size_z = d_ref.shape
    dens = [d_ref[i] for i in range(size_x)]
    mom = [m_ref[i] for i in range(size_x)]
    fuel = [h_ref[i] for i in range(size_x)]
    vel = [a / b for a, b in zip(mom, dens)]
    flux = [a * b + c for a, b, c in zip(mom, vel, dens)]
    carried = [a * b for a, b in zip(fuel, vel)]
    blank = jnp.zeros((8, size_z), jnp.float32)
    for f, rows in enumerate((mom, fuel)):
        for i in range(size_x):
            pad_ref[f, i, 0:8] = blank
            pad_ref[f, i, 8:8 + size_y] = rows[i]
            pad_ref[f, i, 8 + size_y:] = blank
    lane = lanes_of((size_y, size_z))

    def first_diff(rows, i):
        total = jnp.zeros((size_y, size_z), jnp.float32)
        for j, w in enumerate(FIRST_COEFFS, 1):
            if i + j < size_x:
                total = total + w * rows[i + j]
            if i - j >= 0:
                total = total - w * rows[i - j]
        return total

    def second_diffs(f, rows, i):
        here = rows[i]
        total = (3.0 * CENTRE_COEFF) * here
        for j, w in enumerate(SECOND_COEFFS, 1):
            pair = pad_ref[f, i, 8 + j:8 + j + size_y] + pad_ref[f, i, 8 - j:8 - j + size_y]
            pair = pair + jnp.where(lane < size_z - j, pltpu.roll(here, size_z - j, 1), 0.0)
            pair = pair + jnp.where(lane >= j, pltpu.roll(here, j, 1), 0.0)
            if i + j < size_x:
                pair = pair + rows[i + j]
            if i - j >= 0:
                pair = pair + rows[i - j]
            total = total + w * pair
        return total

    for i in range(size_x):
        density_ref[i] = -first_diff(mom, i)
        momentum_ref[i] = VISCOSITY * second_diffs(0, mom, i) - first_diff(flux, i)
        hydrogen_ref[i] = (DIFFUSIVITY * second_diffs(1, fuel, i) - first_diff(carried, i)
                           - fuel[i] * jnp.exp(-ACTIVATION * fuel[i] / dens[i]))
    weight_ref[...] = mode_counts(modes_ref[...])


def edge_kernel(density_part, momentum_part, hydrogen_part, before_ref, after_ref, side_prev_ref,
                side_next_ref, density_ref, momentum_ref, hydrogen_ref, pad_ref):
    size_x, size_y, size_z = density_part.shape

    def outside(ref):
        dens, mom, fuel = ([ref[f, p] for p in range(HALO)] for f in range(3))
        vel = [a / b for a, b in zip(mom, dens)]
        flux = [a * b + c for a, b, c in zip(mom, vel, dens)]
        return mom, flux, fuel, [a * b for a, b in zip(fuel, vel)]

    before, after = outside(before_ref), outside(after_ref)
    row = lax.broadcasted_iota(jnp.int32, (8, size_z), 0)
    blank = jnp.zeros((size_y, size_z), jnp.float32)
    for f in range(2):
        for i in range(size_x):
            pad_ref[f, i, 0:8] = jnp.where(row >= HALO, side_prev_ref[f, i], 0.0)
            pad_ref[f, i, 8:8 + size_y] = blank
            pad_ref[f, i, 8 + size_y:] = jnp.where(row < HALO, side_next_ref[f, i], 0.0)

    def side_part(f, i):
        total = None
        for j, w in enumerate(SECOND_COEFFS, 1):
            pair = pad_ref[f, i, 8 + j:8 + j + size_y] + pad_ref[f, i, 8 - j:8 - j + size_y]
            total = w * pair if total is None else total + w * pair
        return total

    for i in range(size_x):
        density = density_part[i]
        momentum = momentum_part[i] + VISCOSITY * side_part(0, i)
        hydrogen = hydrogen_part[i] + DIFFUSIVITY * side_part(1, i)
        for j, (a, b) in enumerate(zip(FIRST_COEFFS, SECOND_COEFFS), 1):
            for near, at, sign in ((before, i - j + HALO, 1.0), (after, i + j - size_x, -1.0)):
                inside = i - j >= 0 if sign > 0 else i + j < size_x
                if inside:
                    continue
                mom, flux, fuel, carried = (rows[at] for rows in near)
                density = density + (sign * a) * mom
                momentum = momentum + (sign * a) * flux + (VISCOSITY * b) * mom
                hydrogen = hydrogen + (sign * a) * carried + (DIFFUSIVITY * b) * fuel
        density_ref[i] = density
        momentum_ref[i] = momentum
        hydrogen_ref[i] = hydrogen


def post_kernel(cells, d_ref, density_ref, momentum_ref, hydrogen_ref, depth_prev_ref,
                depth_next_ref, parts_ref, weight_ref, plane_ref, line_ref, rot_plane_ref,
                rot_line_ref, density_out, momentum_out, hydrogen_out, buffer_ref, sem):
    size_x, size_y, size_z = d_ref.shape
    send_density = pltpu.make_async_copy(density_ref, density_out, sem.at[2])
    send_density.start()
    lane = lanes_of((size_y, size_z))
    spot = lane % HALO
    late = (lane // HALO) % 2 == 1
    edge = jnp.where(late, depth_prev_ref[...], depth_next_ref[...])
    low_side = SECOND_COEFFS[3] * edge
    high_side = low_side
    for j in (3, 2, 1):
        w = SECOND_COEFFS[j - 1]
        low_side = low_side + jnp.where(spot < j, w * pltpu.roll(edge, size_z - HALO + j, 1), 0.0)
        high_side = high_side + jnp.where(
            spot >= HALO - j, w * pltpu.roll(edge, HALO - j, 1), 0.0)
    edge = jnp.where(late, low_side, high_side)
    rim = (lane < HALO) | (lane >= size_z - HALO)

    def depth_part(f, i):
        at = 2 * HALO * (f * size_x + i)
        return jnp.where(rim, pltpu.roll(edge, (2 * size_z - HALO - at) % size_z, 1), 0.0)

    for i in range(size_x):
        buffer_ref[0, i] = hydrogen_ref[i] + DIFFUSIVITY * depth_part(1, i)
    send_hydrogen = pltpu.make_async_copy(buffer_ref.at[0], hydrogen_out, sem.at[0])
    send_hydrogen.start()

    rot = rotations(rot_plane_ref, rot_line_ref)
    total = jnp.sum(parts_ref[...], axis=0) * (1.0 / cells)
    quad = lanes_of((4, 128)) // 32
    other = swap32(swap64(total))
    waves = jnp.where(quad == 2, -total, total) + jnp.where(quad == 0, -other, other)
    coef = weight_ref[...] * waves
    energy = jnp.sum(coef * waves)
    other = swap32(swap64(coef))
    spec = jnp.where(quad == 2, -coef, coef) + jnp.where(quad == 3, -other, other)
    spec = rot[0] * spec - rot[1] * swap32(spec)
    spec = rot[2] * spec - rot[3] * swap64(spec)
    spec = jnp.concatenate([spec, swap64(spec)], 0)
    mid = lax.dot_general(plane_ref[...], spec, (((1,), (1,)), ((), ())), precision=HIGHEST,
                          preferred_element_type=jnp.float32)
    low = 2.0 * jnp.dot(mid, line_ref[...], precision=HIGHEST, preferred_element_type=jnp.float32)
    force = FORCE_POWER * low.reshape(size_x, size_y, size_z) / (energy + ENERGY_EPS)
    for i in range(size_x):
        part = momentum_ref[i] + VISCOSITY * depth_part(0, i)
        buffer_ref[1, i] = part + d_ref[i] * force[i]
    send_momentum = pltpu.make_async_copy(buffer_ref.at[1], momentum_out, sem.at[1])
    send_momentum.start()
    send_density.wait()
    send_hydrogen.wait()
    send_momentum.wait()


VMEM_SPEC = pl.BlockSpec(memory_space=pltpu.VMEM)
ANY_SPEC = pl.BlockSpec(memory_space=pl.ANY)


def in_vmem(*args):
    return [pltpu.with_memory_space_constraint(a, pltpu.VMEM) for a in args]


def shift(x, axis, step):
    size = lax.axis_size(axis)
    return lax.ppermute(x, axis, [(i, (i + step) % size) for i in range(size)])


def per_device(density, momentum, hydrogen, forced_modes):
    size_x, size_y, size_z = density.shape
    counts = tuple(lax.axis_size(a) for a in AXES)
    devices = math.prod(counts)
    gather = devices <= 64
    slots = devices if gather else 1
    full = tuple(n * c for n, c in zip(density.shape, counts))
    plane = jnp.asarray(plane_table(size_x, size_y, full[0], full[1]))
    line = jnp.asarray(line_table(size_z, full[2]))
    rot_plane, rot_line = (jnp.asarray(t) for t in rotation_tables(counts))
    f32 = jnp.float32
    sources = (density, momentum, plane, line, rot_plane, rot_line, hydrogen, forced_modes.T)
    block = jax.ShapeDtypeStruct(density.shape, f32)
    block_vmem = pltpu.VMEM(density.shape, f32)
    end = pltpu.VMEM((3, HALO, size_y, size_z), f32)
    outs = pl.pallas_call(
        functools.partial(pre_kernel, slots),
        in_specs=[ANY_SPEC] * 8,
        out_specs=[VMEM_SPEC] * 8 + [ANY_SPEC] + [VMEM_SPEC] * 4,
        out_shape=[pltpu.VMEM(a.shape, a.dtype) for a in sources] + [
            jax.ShapeDtypeStruct((slots, 4, 128), f32), end, end,
            pltpu.VMEM((2, size_x, 2 * HALO, size_z), f32), pltpu.VMEM((size_y, 128), f32)],
        scratch_shapes=[pltpu.VMEM((slots, 4, 128), f32), pltpu.SemaphoreType.DMA((8,)),
                        pltpu.SemaphoreType.DMA],
    )(*sources)
    density, momentum, plane, line, rot_plane, rot_line, hydrogen, modes = outs[:8]
    parts, low, high, side, depth = outs[8:]
    if gather:
        parts = lax.all_to_all(parts, AXES, 0, 0)
    else:
        parts = lax.psum(parts, AXES)
    depth_next = shift(depth, "gz", -1)
    depth_prev = depth_next if counts[2] == 2 else shift(depth, "gz", 1)
    after = shift(low, "gx", -1)
    before = shift(high, "gx", 1)
    side_next = shift(side, "gy", -1)
    side_prev = side_next if counts[1] == 2 else shift(side, "gy", 1)
    pad = pltpu.VMEM((2, size_x, 16 + size_y, size_z), f32)
    own = pl.pallas_call(
        local_kernel,
        in_specs=[VMEM_SPEC] * 4,
        out_specs=[VMEM_SPEC] * 4,
        out_shape=[block_vmem] * 3 + [pltpu.VMEM((4, 128), f32)],
        scratch_shapes=[pad],
    )(*in_vmem(density, momentum, hydrogen, modes))
    weight = own[3]
    rates = pl.pallas_call(
        edge_kernel,
        in_specs=[VMEM_SPEC] * 7,
        out_specs=[VMEM_SPEC] * 3,
        out_shape=[block_vmem] * 3,
        scratch_shapes=[pad],
    )(*in_vmem(*own[:3], before, after, side_prev, side_next))
    return tuple(pl.pallas_call(
        functools.partial(post_kernel, float(math.prod(full))),
        in_specs=[VMEM_SPEC] * 12,
        out_specs=[ANY_SPEC] * 3,
        out_shape=[block] * 3,
        scratch_shapes=[pltpu.VMEM((2,) + block.shape, f32), pltpu.SemaphoreType.DMA((3,))],
    )(*in_vmem(density, *rates, depth_prev, depth_next, parts, weight, plane, line,
               rot_plane, rot_line)))


def solution(mesh):
    in_specs = (P("gx", "gy", "gz"), P("gx", "gy", "gz"), P("gx", "gy", "gz"), P())
    out_specs = (P("gx", "gy", "gz"), P("gx", "gy", "gz"), P("gx", "gy", "gz"))
    return jax.shard_map(
        per_device, mesh=mesh, in_specs=in_specs, out_specs=out_specs, check_vma=False
    )
```

profile of v0, /device:TPU:0, one launch (start us, length us, event | category | flops | bytes accessed | tf_op | source)
XLA Modules:
  0.0 20.9 jit_solution(7285441218627122725)
XLA Ops:
  0.6 2.3 %shard_map.103 = (f32[8,16,128]{2,1,0:T(8,128)S(1)}, f32[8,16,128]{2,1,0:T(8,128)S(1)}, f32[128,128]{1,0:T(8,128)S(1)}, f32[8,128]{1,0:T(8,128)S(1)}, f32[8,2,4,...) custom-call(f32[8,16,128]{2,1,0:T(8,128)} %refs_0_.1, ...), custom_call_target="tpu_custom_call" | custom-call | tf_op jit(solution)/shard_map/pallas_call | solution.py:334
  3.0 7.3 %all-to-all-start = ((f32[32,4,128]{2,1,0:T(4,128)}), f32[32,4,128]{2,1,0:T(4,128)S(1)}, u32[]{:S(2)}, u32[]{:S(2)}) async-start(f32[32,4,128]{2,1,0:T(4,128)} %get-tuple-element.37), calls=%async_computation | async-start | bytes 131072 | tf_op jit(solution)/shard_map/all_to_all | solution.py:347
  10.3 0.3 %collective-permute-start = (f32[3,4,16,128]{3,2,1,0:T(8,128)S(1)}, f32[3,4,16,128]{3,2,1,0:T(8,128)S(1)}, u32[]{:S(2)}, u32[]{:S(2)}) collective-permute-start(f32[3,4,16,128]{3,2,1,0:T(8,128)S(1)} %get-tuple-element.30), channel_id=1, source_target_pairs={{0,8},{8,16},{16,24},{24,0},{1,9},{9,17},{17,25},{25,1},{2,10},{10... | collective-permute-start | bytes 294920 | tf_op jit(solution)/shard_map/ppermute | solution.py:316
  10.6 1.5 %collective-permute-start.1 = (f32[3,4,16,128]{3,2,1,0:T(8,128)S(1)}, f32[3,4,16,128]{3,2,1,0:T(8,128)S(1)}, u32[]{:S(2)}, u32[]{:S(2)}) collective-permute-start(f32[3,4,16,128]{3,2,1,0:T(8,128)S(1)} %get-tuple-element.31), channel_id=1, source_target_pairs={{0,24},{8,0},{16,8},{24,16},{1,25},{9,1},{17,9},{25,17},{2,26},{10... | collective-permute-start | bytes 294920 | tf_op jit(solution)/shard_map/ppermute | solution.py:316
  12.1 1.8 %collective-permute-start.2 = (f32[2,8,8,128]{3,2,1,0:T(8,128)S(1)}, f32[2,8,8,128]{3,2,1,0:T(8,128)S(1)}, u32[]{:S(2)}, u32[]{:S(2)}) collective-permute-start(f32[2,8,8,128]{3,2,1,0:T(8,128)S(1)} %get-tuple-element.32), channel_id=1, source_target_pairs={{0,4},{4,0},{1,5},{5,1},{2,6},{6,2},{3,7},{7,3},{8,12},{12,8},{9,1... | collective-permute-start | bytes 196616 | tf_op jit(solution)/shard_map/ppermute | solution.py:316
  13.9 1.5 %collective-permute-start.3 = (f32[16,128]{1,0:T(8,128)S(1)}, f32[16,128]{1,0:T(8,128)S(1)}, u32[]{:S(2)}, u32[]{:S(2)}) collective-permute-start(f32[16,128]{1,0:T(8,128)S(1)} %get-tuple-element.36), channel_id=1, source_target_pairs={{0,1},{1,2},{2,3},{3,0},{4,5},{5,6},{6,7},{7,4},{8,9},{9,10},{10,1... | collective-permute-start | bytes 24584 | tf_op jit(solution)/shard_map/ppermute | solution.py:316
  15.3 2.4 %collective-permute-start.4 = (f32[16,128]{1,0:T(8,128)S(1)}, f32[16,128]{1,0:T(8,128)S(1)}, u32[]{:S(2)}, u32[]{:S(2)}) collective-permute-start(f32[16,128]{1,0:T(8,128)S(1)} %get-tuple-element.36), channel_id=1, source_target_pairs={{0,3},{1,0},{2,1},{3,2},{4,7},{5,4},{6,5},{7,6},{8,11},{9,8},{10,9... | collective-permute-start | bytes 24584 | tf_op jit(solution)/shard_map/ppermute | solution.py:316
  17.7 0.3 %shard_map.104 = (f32[8,16,128]{2,1,0:T(8,128)S(1)}, f32[8,16,128]{2,1,0:T(8,128)S(1)}, f32[8,16,128]{2,1,0:T(8,128)S(1)}, f32[4,128]{1,0:T(4,128)S(1)}) custom-call(f32[8,16,128]{2,1,0:T(8,128)S(1)} %get-tuple-element.23.d_ref, f32[8,16,128]{2,1,0:T(8,128)S(1)} %get-tuple-element.24.m_ref, f32[8,16,128]{2,1,0:T(8,128)S(1)} %get-tuple-element.25.h_ref, ...), custom_call_target="tpu_custom_call" | custom-call | tf_op jit(solution)/shard_map/pallas_call | solution.py:357
  18.1 0.0 collective-permute-done.2.side_prev_ref.side_next_ref
  18.1 0.0 collective-permute-done.before_ref
  18.1 0.0 collective-permute-done.1.after_ref
  18.1 0.2 shard_map.105
  18.2 1.1 %collective-permute-done.3.depth_prev_ref = f32[16,128]{1,0:T(8,128)S(1)} collective-permute-done((f32[16,128]{1,0:T(8,128)S(1)}, f32[16,128]{1,0:T(8,128)S(1)}, u32[]{:S(2)}, u32[]{:S(2)}) %collective-permute-start.3) | collective-permute-done | bytes 8224 | tf_op jit(solution)/shard_map/ppermute | solution.py:316
  19.3 0.0 collective-permute-done.4.depth_next_ref
  19.3 0.0 all-to-all-done.parts_ref
  19.3 1.6 %shard_map.106 = (f32[8,16,128]{2,1,0:T(8,128)}, f32[8,16,128]{2,1,0:T(8,128)}, f32[8,16,128]{2,1,0:T(8,128)}) custom-call(f32[8,16,128]{2,1,0:T(8,128)S(1)} %get-tuple-element.23.d_ref, f32[8,16,128]{2,1,0:T(8,128)S(1)} %get-tuple-element.33.density_ref, f32[8,16,128]{2,1,0:T(8,128)S(1)} %get-tuple-element.34.momentum_ref, ...), custom_call_target="tpu_custom_call" | custom-call | tf_op jit(solution)/shard_map/pallas_call | solution.py:372
Async XLA Ops:
  3.0 16.4 %all-to-all-start = ((f32[32,4,128]{2,1,0:T(4,128)}), f32[32,4,128]{2,1,0:T(4,128)S(1)}, u32[]{:S(2)}, u32[]{:S(2)}) async-start(f32[32,4,128]{2,1,0:T(4,128)} %get-tuple-element.37), calls=%async_computation | async-start | bytes 131072 | tf_op jit(solution)/shard_map/all_to_all | solution.py:347
  10.3 7.8 %collective-permute-start = (f32[3,4,16,128]{3,2,1,0:T(8,128)S(1)}, f32[3,4,16,128]{3,2,1,0:T(8,128)S(1)}, u32[]{:S(2)}, u32[]{:S(2)}) collective-permute-start(f32[3,4,16,128]{3,2,1,0:T(8,128)S(1)} %get-tuple-element.30), channel_id=1, source_target_pairs={{0,8},{8,16},{16,24},{24,0},{1,9},{9,17},{17,25},{25,1},{2,10},{10... | collective-permute-start | bytes 294920 | tf_op jit(solution)/shard_map/ppermute | solution.py:316
  10.6 7.5 %collective-permute-start.1 = (f32[3,4,16,128]{3,2,1,0:T(8,128)S(1)}, f32[3,4,16,128]{3,2,1,0:T(8,128)S(1)}, u32[]{:S(2)}, u32[]{:S(2)}) collective-permute-start(f32[3,4,16,128]{3,2,1,0:T(8,128)S(1)} %get-tuple-element.31), channel_id=1, source_target_pairs={{0,24},{8,0},{16,8},{24,16},{1,25},{9,1},{17,9},{25,17},{2,26},{10... | collective-permute-start | bytes 294920 | tf_op jit(solution)/shard_map/ppermute | solution.py:316
  12.1 5.9 %collective-permute-start.2 = (f32[2,8,8,128]{3,2,1,0:T(8,128)S(1)}, f32[2,8,8,128]{3,2,1,0:T(8,128)S(1)}, u32[]{:S(2)}, u32[]{:S(2)}) collective-permute-start(f32[2,8,8,128]{3,2,1,0:T(8,128)S(1)} %get-tuple-element.32), channel_id=1, source_target_pairs={{0,4},{4,0},{1,5},{5,1},{2,6},{6,2},{3,7},{7,3},{8,12},{12,8},{9,1... | collective-permute-start | bytes 196616 | tf_op jit(solution)/shard_map/ppermute | solution.py:316
  13.9 5.4 %collective-permute-start.3 = (f32[16,128]{1,0:T(8,128)S(1)}, f32[16,128]{1,0:T(8,128)S(1)}, u32[]{:S(2)}, u32[]{:S(2)}) collective-permute-start(f32[16,128]{1,0:T(8,128)S(1)} %get-tuple-element.36), channel_id=1, source_target_pairs={{0,1},{1,2},{2,3},{3,0},{4,5},{5,6},{6,7},{7,4},{8,9},{9,10},{10,1... | collective-permute-start | bytes 24584 | tf_op jit(solution)/shard_map/ppermute | solution.py:316
  15.3 4.0 %collective-permute-start.4 = (f32[16,128]{1,0:T(8,128)S(1)}, f32[16,128]{1,0:T(8,128)S(1)}, u32[]{:S(2)}, u32[]{:S(2)}) collective-permute-start(f32[16,128]{1,0:T(8,128)S(1)} %get-tuple-element.36), channel_id=1, source_target_pairs={{0,3},{1,0},{2,1},{3,2},{4,7},{5,4},{6,5},{7,6},{8,11},{9,8},{10,9... | collective-permute-start | bytes 24584 | tf_op jit(solution)/shard_map/ppermute | solution.py:316
where the time goes:
time: 21.1 us; the launch traced here: 20.9 us
  starting transfers between devices  14.7 us (70%)
  Pallas kernels  4.44 us (21%)
  waiting for transfers between devices  1.09 us (5%)
  between operations  0.69 us (3%)
    ppermute x5, starting transfers between devices, shift(): return lax.ppermute(x, axis, [(i, (i + step) % size) for i in range(size)])  7.39 us
    all_to_all x1, starting transfers between devices, per_device(): parts = lax.all_to_all(parts, AXES, 0, 0)  7.33 us
    pallas_call x1, Pallas kernels, per_device(): pl.pallas_call(functools.partial(pre_kernel, slots), in_specs=[ANY_SPEC]...  2.34 us
    pallas_call x1, Pallas kernels, per_device(): pl.pallas_call(functools.partial(post_kernel, float(math.prod(full))), in...  1.6 us
    ppermute x5, waiting for transfers between devices, shift(): return lax.ppermute(x, axis, [(i, (i + step) % size) for i in range(size)])  1.09 us
  transfers between devices with their start and end apart: 6, of which 1 were waited for; matrix products, arithmetic and copies ran while one was open for 0% of the time, Pallas kernels for 2%

commit v1 on v0

--- a/solution.py
+++ b/solution.py
@@ -29,57 +29,55 @@
 ]
 
 
-def plane_table(local_x, local_y, full_x, full_y):
-    x = np.arange(local_x)[:, None]
-    y = np.arange(local_y)[None, :]
-    table = np.zeros((local_x * local_y, 128), np.float64)
-    for lane, (kx, ky) in enumerate(HALF_PLANE):
-        angle = 2.0 * np.pi * (kx * x / full_x + ky * y / full_y)
-        table[:, lane] = np.cos(angle).reshape(-1)
-        table[:, 32 + lane] = np.sin(angle).reshape(-1)
+def plane_tables(local, counts):
+    full_x, full_y = local[0] * counts[0], local[1] * counts[1]
+    table = np.zeros((counts[0], counts[1], 64, local[0], local[1]), np.float64)
+    for i in range(counts[0]):
+        for j in range(counts[1]):
+            x = (i * local[0] + np.arange(local[0]))[:, None]
+            y = (j * local[1] + np.arange(local[1]))[None, :]
+            for row, (kx, ky) in enumerate(HALF_PLANE):
+                angle = 2.0 * np.pi * ((kx * x % full_x) / full_x + (ky * y % full_y) / full_y)
+                table[i, j, row] = np.cos(angle)
+                table[i, j, 32 + row] = np.sin(angle)
+    return table.reshape(counts[0] * counts[1], 64, -1).astype(np.float32)
+
+
+def line_tables(local_z, count):
+    full_z = local_z * count
+    table = np.zeros((count, 8, local_z), np.float64)
+    for i in range(count):
+        z = i * local_z + np.arange(local_z)
+        for kz in range(KMAX + 1):
+            angle = 2.0 * np.pi * (kz * z % full_z) / full_z
+            table[i, kz] = np.cos(angle)
+            table[i, 4 + kz] = np.sin(angle)
     return table.astype(np.float32)
 
 
-def line_table(local_z, full_z):
-    z = np.arange(local_z)
-    table = np.zeros((8, local_z), np.float64)
-    for kz in range(KMAX + 1):
-        angle = 2.0 * np.pi * kz * z / full_z
-        table[kz] = np.cos(angle)
-        table[4 + kz] = np.sin(angle)
-    return table.astype(np.float32)
-
-
-def rotation_tables(counts):
-    count_x, count_y, count_z = counts
-    lane = np.arange(128)
-    wave = lane % 32
-    kx = np.array([HALF_PLANE[w][0] if w < len(HALF_PLANE) else 0 for w in wave])
-    ky = np.array([HALF_PLANE[w][1] if w < len(HALF_PLANE) else 0 for w in wave])
-    sign_xy = np.where(lane & 32, 1.0, -1.0)
-    sign_z = np.where(lane & 64, 1.0, -1.0)
-    plane = np.zeros((count_x, count_y, 2, 4, 128))
-    for i in range(count_x):
-        for j in range(count_y):
-            angle = 2.0 * np.pi * ((kx * i % count_x) / count_x + (ky * j % count_y) / count_y)
-            plane[i, j, 0] = np.cos(angle)
-            plane[i, j, 1] = np.sin(angle) * sign_xy
-    line = np.zeros((count_z, 2, 4, 128))
-    for k in range(count_z):
-        angle = 2.0 * np.pi * ((np.arange(4) * k) % count_z) / count_z
-        line[k, 0] = np.cos(angle)[:, None]
-        line[k, 1] = np.sin(angle)[:, None] * sign_z[None, :]
-    plane = plane.reshape(count_x * count_y, 2, 4, 128)
-    return plane.astype(np.float32), line.astype(np.float32)
+def deep_tables(table):
+    pieces = []
+    rest = jnp.asarray(table)
+    for _ in range(3):
+        piece = rest.astype(jnp.bfloat16)
+        pieces.append(piece)
+        rest = rest - piece.astype(jnp.float32)
+    return jnp.concatenate([pieces[n] for n in (0, 1, 2, 0, 1, 0)], 1)
 
 
 def lanes_of(shape):
     return lax.broadcasted_iota(jnp.int32, shape, len(shape) - 1)
 
 
-def swap32(a):
-    bit = (lanes_of(a.shape) & 32) != 0
-    return jnp.where(bit, pltpu.roll(a, 32, 1), pltpu.roll(a, 96, 1))
+def split(a):
+    high = a.astype(jnp.bfloat16).astype(jnp.float32)
+    rest = a - high
+    mid = rest.astype(jnp.bfloat16).astype(jnp.float32)
+    return high, mid, rest - mid
+
+
+def four_quadrants(plane):
+    return jnp.concatenate([plane, plane[32:64], plane[0:32]], 0)
 
 
 def swap64(a):
@@ -94,32 +92,30 @@
     return copies
 
 
-def rotations(plane_ref, line_ref):
+def pre_kernel(slots, *refs):
+    sources, targets = list(refs[:7]), list(refs[7:13])
+    part_out, low_ref, high_ref, side_ref, depth_ref, line_ref, part_ref, sems, part_sem = refs[13:]
+    targets.insert(2, line_ref)
     place = lax.axis_index("gx") * lax.axis_size("gy") + lax.axis_index("gy")
     level = lax.axis_index("gz")
-    return plane_ref[place, 0], plane_ref[place, 1], line_ref[level, 0], line_ref[level, 1]
-
-
-def pre_kernel(slots, *refs):
-    sources, targets = refs[:8], refs[8:16]
-    part_out, low_ref, high_ref, side_ref, depth_ref, part_ref, sems, part_sem = refs[16:]
+    sources[2:4] = sources[2].at[level], sources[3].at[place]
+    sources[5] = sources[5].at[level]
     copies = fetch_all(sources, targets, sems)
-    d_ref, m_ref, plane_ref, line_ref, rot_plane_ref, rot_line_ref, h_ref, _ = targets
+    d_ref, m_ref, _, plane_ref, h_ref = targets[:5]
     size_x, size_y, size_z = d_ref.shape
-    for copy in copies[:6]:
+    for copy in copies[:4]:
         copy.wait()
-    rot = rotations(rot_plane_ref, rot_line_ref)
     flat = (m_ref[...] / d_ref[...]).reshape(size_x * size_y, size_z)
-    along = lax.dot_general(line_ref[...], flat, (((1,), (1,)), ((), ())), precision=HIGHEST,
+    across = (((1,), (1,)), ((), ()))
+    along = lax.dot_general(line_ref[...], flat, across, precision=HIGHEST,
                             preferred_element_type=jnp.float32)
-    both = jnp.dot(along, plane_ref[...], precision=HIGHEST, preferred_element_type=jnp.float32)
-    part = both[0:4] + swap64(both)[4:8]
-    part = rot[0] * part + rot[1] * swap32(part)
-    part = rot[2] * part + rot[3] * swap64(part)
+    both = lax.dot_general(along, four_quadrants(plane_ref[...]), across, precision=HIGHEST,
+                           preferred_element_type=jnp.float32)
+    part = jnp.where(lanes_of((4, 128)) < 64, both[0:4], both[4:8])
     part_ref[...] = jnp.broadcast_to(part[None], (slots, 4, 128))
     send = pltpu.make_async_copy(part_ref, part_out, part_sem)
     send.start()
-    for copy in copies[6:]:
+    for copy in copies[4:]:
         copy.wait()
     for index, ref in enumerate((d_ref, m_ref, h_ref)):
         low_ref[index] = ref[0:HALO]
@@ -249,8 +245,8 @@
 
 
 def post_kernel(cells, d_ref, density_ref, momentum_ref, hydrogen_ref, depth_prev_ref,
-                depth_next_ref, parts_ref, weight_ref, plane_ref, line_ref, rot_plane_ref,
-                rot_line_ref, density_out, momentum_out, hydrogen_out, buffer_ref, sem):
+                depth_next_ref, parts_ref, weight_ref, plane_ref, line_ref, density_out,
+                momentum_out, hydrogen_out, buffer_ref, sem):
     size_x, size_y, size_z = d_ref.shape
     send_density = pltpu.make_async_copy(density_ref, density_out, sem.at[2])
     send_density.start()
@@ -277,22 +273,27 @@
     send_hydrogen = pltpu.make_async_copy(buffer_ref.at[0], hydrogen_out, sem.at[0])
     send_hydrogen.start()
 
-    rot = rotations(rot_plane_ref, rot_line_ref)
-    total = jnp.sum(parts_ref[...], axis=0) * (1.0 / cells)
+    parts = [parts_ref[n] for n in range(parts_ref.shape[0])]
+    while len(parts) > 1:
+        half = len(parts) // 2
+        parts = [a + b for a, b in zip(parts[:half], parts[half:])] + parts[2 * half:]
+    total = parts[0] * (1.0 / cells)
     quad = lanes_of((4, 128)) // 32
-    other = swap32(swap64(total))
-    waves = jnp.where(quad == 2, -total, total) + jnp.where(quad == 0, -other, other)
+    other = swap64(total)
+    waves = jnp.where(quad == 3, -total, total) + jnp.where(quad == 0, -other, other)
     coef = weight_ref[...] * waves
     energy = jnp.sum(coef * waves)
-    other = swap32(swap64(coef))
-    spec = jnp.where(quad == 2, -coef, coef) + jnp.where(quad == 3, -other, other)
-    spec = rot[0] * spec - rot[1] * swap32(spec)
-    spec = rot[2] * spec - rot[3] * swap64(spec)
-    spec = jnp.concatenate([spec, swap64(spec)], 0)
-    mid = lax.dot_general(plane_ref[...], spec, (((1,), (1,)), ((), ())), precision=HIGHEST,
+    other = swap64(coef)
+    spec = jnp.where(quad == 3, -coef, coef) + jnp.where(quad == 2, -other, other)
+    spec = jnp.concatenate([jnp.where(quad < 2, spec, 0.0), jnp.where(quad < 2, 0.0, spec)], 0)
+    mid = jnp.dot(spec, four_quadrants(plane_ref[...]), precision=HIGHEST,
+                  preferred_element_type=jnp.float32)
+    high, middle, rest = split(mid)
+    mid = jnp.concatenate([high, high, high, middle, middle, rest], 0).astype(jnp.bfloat16)
+    low = lax.dot_general(mid, line_ref[...], (((0,), (0,)), ((), ())),
                           preferred_element_type=jnp.float32)
-    low = 2.0 * jnp.dot(mid, line_ref[...], precision=HIGHEST, preferred_element_type=jnp.float32)
-    force = FORCE_POWER * low.reshape(size_x, size_y, size_z) / (energy + ENERGY_EPS)
+    scale = 2.0 * FORCE_POWER / (energy + ENERGY_EPS)
+    force = low.reshape(size_x, size_y, size_z) * scale
     for i in range(size_x):
         part = momentum_ref[i] + VISCOSITY * depth_part(0, i)
         buffer_ref[1, i] = part + d_ref[i] * force[i]
@@ -323,26 +324,29 @@
     gather = devices <= 64
     slots = devices if gather else 1
     full = tuple(n * c for n, c in zip(density.shape, counts))
-    plane = jnp.asarray(plane_table(size_x, size_y, full[0], full[1]))
-    line = jnp.asarray(line_table(size_z, full[2]))
-    rot_plane, rot_line = (jnp.asarray(t) for t in rotation_tables(counts))
+    plane = jnp.asarray(plane_tables(density.shape, counts))
+    line = line_tables(size_z, counts[2])
+    deep = deep_tables(line)
     f32 = jnp.float32
-    sources = (density, momentum, plane, line, rot_plane, rot_line, hydrogen, forced_modes.T)
+    sources = (density, momentum, jnp.asarray(line), plane, hydrogen, deep, forced_modes.T)
+    kept = [pltpu.VMEM(a.shape[1:] if n in (3, 5) else a.shape, a.dtype)
+            for n, a in enumerate(sources) if n != 2]
     block = jax.ShapeDtypeStruct(density.shape, f32)
     block_vmem = pltpu.VMEM(density.shape, f32)
     end = pltpu.VMEM((3, HALO, size_y, size_z), f32)
     outs = pl.pallas_call(
         functools.partial(pre_kernel, slots),
-        in_specs=[ANY_SPEC] * 8,
-        out_specs=[VMEM_SPEC] * 8 + [ANY_SPEC] + [VMEM_SPEC] * 4,
-        out_shape=[pltpu.VMEM(a.shape, a.dtype) for a in sources] + [
+        in_specs=[ANY_SPEC] * 7,
+        out_specs=[VMEM_SPEC] * 6 + [ANY_SPEC] + [VMEM_SPEC] * 4,
+        out_shape=kept + [
             jax.ShapeDtypeStruct((slots, 4, 128), f32), end, end,
             pltpu.VMEM((2, size_x, 2 * HALO, size_z), f32), pltpu.VMEM((size_y, 128), f32)],
-        scratch_shapes=[pltpu.VMEM((slots, 4, 128), f32), pltpu.SemaphoreType.DMA((8,)),
+        scratch_shapes=[pltpu.VMEM(line.shape[1:], f32), pltpu.VMEM((slots, 4, 128), f32),
+                        pltpu.SemaphoreType.DMA((7,)),
                         pltpu.SemaphoreType.DMA],
     )(*sources)
-    density, momentum, plane, line, rot_plane, rot_line, hydrogen, modes = outs[:8]
-    parts, low, high, side, depth = outs[8:]
+    density, momentum, plane, hydrogen, deep, modes = outs[:6]
+    parts, low, high, side, depth = outs[6:]
     if gather:
         parts = lax.all_to_all(parts, AXES, 0, 0)
     else:
@@ -371,12 +375,11 @@
     )(*in_vmem(*own[:3], before, after, side_prev, side_next))
     return tuple(pl.pallas_call(
         functools.partial(post_kernel, float(math.prod(full))),
-        in_specs=[VMEM_SPEC] * 12,
+        in_specs=[VMEM_SPEC] * 10,
         out_specs=[ANY_SPEC] * 3,
         out_shape=[block] * 3,
         scratch_shapes=[pltpu.VMEM((2,) + block.shape, f32), pltpu.SemaphoreType.DMA((3,))],
-    )(*in_vmem(density, *rates, depth_prev, depth_next, parts, weight, plane, line,
-               rot_plane, rot_line)))
+    )(*in_vmem(density, *rates, depth_prev, depth_next, parts, weight, plane, deep)))
 
 
 def solution(mesh):

time: 21.1 us -> 20.6 us (0.976)
  Pallas kernels: 4.44 us -> 3.91 us
    pallas_call x1, Pallas kernels: 1.6 us -> 1.2 us  [per_device(): pl.pallas_call(functools.partial(post_kernel, float(math.prod(full))), in...]
where the time goes in v1:
time: 20.6 us; the launch traced here: 20.4 us
  starting transfers between devices  14.7 us (71%)
  Pallas kernels  3.91 us (19%)
  waiting for transfers between devices  1.09 us (5%)
  between operations  0.68 us (3%)
    ppermute x5, starting transfers between devices, shift(): return lax.ppermute(x, axis, [(i, (i + step) % size) for i in range(size)])  7.39 us
    all_to_all x1, starting transfers between devices, per_device(): parts = lax.all_to_all(parts, AXES, 0, 0)  7.33 us
    pallas_call x1, Pallas kernels, per_device(): pl.pallas_call(functools.partial(pre_kernel, slots), in_specs=[ANY_SPEC]...  2.2 us
    pallas_call x1, Pallas kernels, per_device(): pl.pallas_call(functools.partial(post_kernel, float(math.prod(full))), in...  1.2 us
    ppermute x5, waiting for transfers between devices, shift(): return lax.ppermute(x, axis, [(i, (i + step) % size) for i in range(size)])  1.09 us
  transfers between devices with their start and end apart: 6, of which 1 were waited for; matrix products, arithmetic and copies ran while one was open for 0% of the time, Pallas kernels for 2%

profile of v1, /device:TPU:0, one launch (start us, length us, event | category | flops | bytes accessed | tf_op | source)
XLA Modules:
  0.0 20.4 jit_solution(13127323209246416952)
XLA Ops:
  0.6 2.2 %shard_map.85 = (f32[8,16,128]{2,1,0:T(8,128)S(1)}, f32[8,16,128]{2,1,0:T(8,128)S(1)}, f32[64,128]{1,0:T(8,128)S(1)}, f32[8,16,128]{2,1,0:T(8,128)S(1)}, bf16[48...) custom-call(f32[8,16,128]{2,1,0:T(8,128)} %refs_0_.1, ...), custom_call_target="tpu_custom_call" | custom-call | tf_op jit(solution)/shard_map/pallas_call | solution.py:337
  2.8 7.3 %all-to-all-start = ((f32[32,4,128]{2,1,0:T(4,128)}), f32[32,4,128]{2,1,0:T(4,128)S(1)}, u32[]{:S(2)}, u32[]{:S(2)}) async-start(f32[32,4,128]{2,1,0:T(4,128)} %get-tuple-element.35), calls=%async_computation | async-start | bytes 131072 | tf_op jit(solution)/shard_map/all_to_all | solution.py:351
  10.2 0.3 %collective-permute-start = (f32[3,4,16,128]{3,2,1,0:T(8,128)S(1)}, f32[3,4,16,128]{3,2,1,0:T(8,128)S(1)}, u32[]{:S(2)}, u32[]{:S(2)}) collective-permute-start(f32[3,4,16,128]{3,2,1,0:T(8,128)S(1)} %get-tuple-element.28), channel_id=1, source_target_pairs={{0,8},{8,16},{16,24},{24,0},{1,9},{9,17},{17,25},{25,1},{2,10},{10... | collective-permute-start | bytes 294920 | tf_op jit(solution)/shard_map/ppermute | solution.py:317
  10.5 1.5 %collective-permute-start.1 = (f32[3,4,16,128]{3,2,1,0:T(8,128)S(1)}, f32[3,4,16,128]{3,2,1,0:T(8,128)S(1)}, u32[]{:S(2)}, u32[]{:S(2)}) collective-permute-start(f32[3,4,16,128]{3,2,1,0:T(8,128)S(1)} %get-tuple-element.29), channel_id=1, source_target_pairs={{0,24},{8,0},{16,8},{24,16},{1,25},{9,1},{17,9},{25,17},{2,26},{10... | collective-permute-start | bytes 294920 | tf_op jit(solution)/shard_map/ppermute | solution.py:317
  12.0 1.8 %collective-permute-start.2 = (f32[2,8,8,128]{3,2,1,0:T(8,128)S(1)}, f32[2,8,8,128]{3,2,1,0:T(8,128)S(1)}, u32[]{:S(2)}, u32[]{:S(2)}) collective-permute-start(f32[2,8,8,128]{3,2,1,0:T(8,128)S(1)} %get-tuple-element.30), channel_id=1, source_target_pairs={{0,4},{4,0},{1,5},{5,1},{2,6},{6,2},{3,7},{7,3},{8,12},{12,8},{9,1... | collective-permute-start | bytes 196616 | tf_op jit(solution)/shard_map/ppermute | solution.py:317
  13.7 1.5 %collective-permute-start.3 = (f32[16,128]{1,0:T(8,128)S(1)}, f32[16,128]{1,0:T(8,128)S(1)}, u32[]{:S(2)}, u32[]{:S(2)}) collective-permute-start(f32[16,128]{1,0:T(8,128)S(1)} %get-tuple-element.34), channel_id=1, source_target_pairs={{0,1},{1,2},{2,3},{3,0},{4,5},{5,6},{6,7},{7,4},{8,9},{9,10},{10,1... | collective-permute-start | bytes 24584 | tf_op jit(solution)/shard_map/ppermute | solution.py:317
  15.2 2.4 %collective-permute-start.4 = (f32[16,128]{1,0:T(8,128)S(1)}, f32[16,128]{1,0:T(8,128)S(1)}, u32[]{:S(2)}, u32[]{:S(2)}) collective-permute-start(f32[16,128]{1,0:T(8,128)S(1)} %get-tuple-element.34), channel_id=1, source_target_pairs={{0,3},{1,0},{2,1},{3,2},{4,7},{5,4},{6,5},{7,6},{8,11},{9,8},{10,9... | collective-permute-start | bytes 24584 | tf_op jit(solution)/shard_map/ppermute | solution.py:317
  17.6 0.4 %shard_map.86 = (f32[8,16,128]{2,1,0:T(8,128)S(1)}, f32[8,16,128]{2,1,0:T(8,128)S(1)}, f32[8,16,128]{2,1,0:T(8,128)S(1)}, f32[4,128]{1,0:T(4,128)S(1)}) custom-call(f32[8,16,128]{2,1,0:T(8,128)S(1)} %get-tuple-element.21.d_ref, f32[8,16,128]{2,1,0:T(8,128)S(1)} %get-tuple-element.22.m_ref, f32[8,16,128]{2,1,0:T(8,128)S(1)} %get-tuple-element.23.h_ref, ...), custom_call_target="tpu_custom_call" | custom-call | tf_op jit(solution)/shard_map/pallas_call | solution.py:361
  17.9 0.0 collective-permute-done.2.side_prev_ref.side_next_ref
  17.9 0.0 collective-permute-done.before_ref
  17.9 0.0 collective-permute-done.1.after_ref
  18.0 0.2 shard_map.87
  18.1 1.1 %collective-permute-done.3.depth_prev_ref = f32[16,128]{1,0:T(8,128)S(1)} collective-permute-done((f32[16,128]{1,0:T(8,128)S(1)}, f32[16,128]{1,0:T(8,128)S(1)}, u32[]{:S(2)}, u32[]{:S(2)}) %collective-permute-start.3) | collective-permute-done | bytes 8224 | tf_op jit(solution)/shard_map/ppermute | solution.py:317
  19.2 0.0 collective-permute-done.4.depth_next_ref
  19.2 0.0 all-to-all-done.parts_ref
  19.2 1.2 %shard_map.88 = (f32[8,16,128]{2,1,0:T(8,128)}, f32[8,16,128]{2,1,0:T(8,128)}, f32[8,16,128]{2,1,0:T(8,128)}) custom-call(f32[8,16,128]{2,1,0:T(8,128)S(1)} %get-tuple-element.21.d_ref, f32[8,16,128]{2,1,0:T(8,128)S(1)} %get-tuple-element.31.density_ref, f32[8,16,128]{2,1,0:T(8,128)S(1)} %get-tuple-element.32.momentum_ref, ...), custom_call_target="tpu_custom_call" | custom-call | tf_op jit(solution)/shard_map/pallas_call | solution.py:376
Async XLA Ops:
  2.8 16.4 %all-to-all-start = ((f32[32,4,128]{2,1,0:T(4,128)}), f32[32,4,128]{2,1,0:T(4,128)S(1)}, u32[]{:S(2)}, u32[]{:S(2)}) async-start(f32[32,4,128]{2,1,0:T(4,128)} %get-tuple-element.35), calls=%async_computation | async-start | bytes 131072 | tf_op jit(solution)/shard_map/all_to_all | solution.py:351
  10.2 7.8 %collective-permute-start = (f32[3,4,16,128]{3,2,1,0:T(8,128)S(1)}, f32[3,4,16,128]{3,2,1,0:T(8,128)S(1)}, u32[]{:S(2)}, u32[]{:S(2)}) collective-permute-start(f32[3,4,16,128]{3,2,1,0:T(8,128)S(1)} %get-tuple-element.28), channel_id=1, source_target_pairs={{0,8},{8,16},{16,24},{24,0},{1,9},{9,17},{17,25},{25,1},{2,10},{10... | collective-permute-start | bytes 294920 | tf_op jit(solution)/shard_map/ppermute | solution.py:317
  10.5 7.5 %collective-permute-start.1 = (f32[3,4,16,128]{3,2,1,0:T(8,128)S(1)}, f32[3,4,16,128]{3,2,1,0:T(8,128)S(1)}, u32[]{:S(2)}, u32[]{:S(2)}) collective-permute-start(f32[3,4,16,128]{3,2,1,0:T(8,128)S(1)} %get-tuple-element.29), channel_id=1, source_target_pairs={{0,24},{8,0},{16,8},{24,16},{1,25},{9,1},{17,9},{25,17},{2,26},{10... | collective-permute-start | bytes 294920 | tf_op jit(solution)/shard_map/ppermute | solution.py:317
  12.0 6.0 %collective-permute-start.2 = (f32[2,8,8,128]{3,2,1,0:T(8,128)S(1)}, f32[2,8,8,128]{3,2,1,0:T(8,128)S(1)}, u32[]{:S(2)}, u32[]{:S(2)}) collective-permute-start(f32[2,8,8,128]{3,2,1,0:T(8,128)S(1)} %get-tuple-element.30), channel_id=1, source_target_pairs={{0,4},{4,0},{1,5},{5,1},{2,6},{6,2},{3,7},{7,3},{8,12},{12,8},{9,1... | collective-permute-start | bytes 196616 | tf_op jit(solution)/shard_map/ppermute | solution.py:317
  13.7 5.4 %collective-permute-start.3 = (f32[16,128]{1,0:T(8,128)S(1)}, f32[16,128]{1,0:T(8,128)S(1)}, u32[]{:S(2)}, u32[]{:S(2)}) collective-permute-start(f32[16,128]{1,0:T(8,128)S(1)} %get-tuple-element.34), channel_id=1, source_target_pairs={{0,1},{1,2},{2,3},{3,0},{4,5},{5,6},{6,7},{7,4},{8,9},{9,10},{10,1... | collective-permute-start | bytes 24584 | tf_op jit(solution)/shard_map/ppermute | solution.py:317
  15.2 4.0 %collective-permute-start.4 = (f32[16,128]{1,0:T(8,128)S(1)}, f32[16,128]{1,0:T(8,128)S(1)}, u32[]{:S(2)}, u32[]{:S(2)}) collective-permute-start(f32[16,128]{1,0:T(8,128)S(1)} %get-tuple-element.34), channel_id=1, source_target_pairs={{0,3},{1,0},{2,1},{3,2},{4,7},{5,4},{6,5},{7,6},{8,11},{9,8},{10,9... | collective-permute-start | bytes 24584 | tf_op jit(solution)/shard_map/ppermute | solution.py:317

commit v2 on v1

--- a/solution.py
+++ b/solution.py
@@ -22,7 +22,6 @@
 FORCE_POWER = 0.3
 ENERGY_EPS = 1e-06
 ACTIVATION = 2.0
-HIGHEST = lax.Precision.HIGHEST
 
 HALF_PLANE = [(0, ky) for ky in range(KMAX + 1)] + [
     (kx, ky) for kx in range(1, KMAX + 1) for ky in range(-KMAX, KMAX + 1)
@@ -76,6 +75,22 @@
     return high, mid, rest - mid
 
 
+def stacked_rows(a):
+    high, mid, low = split(a)
+    blank = jnp.zeros_like(a)
+    rows = [jnp.concatenate(r, 1) for r in (
+        (high, high, high), (mid, mid, blank), (low, blank, blank), (blank, blank, blank))]
+    return jnp.concatenate(rows, 0).astype(jnp.bfloat16)
+
+
+def stacked_columns(a):
+    return jnp.concatenate(split(a), 1).astype(jnp.bfloat16)
+
+
+def fold(a):
+    return (a[16:24] + a[8:16]) + a[0:8]
+
+
 def four_quadrants(plane):
     return jnp.concatenate([plane, plane[32:64], plane[0:32]], 0)
 
@@ -87,8 +102,8 @@
 def fetch_all(sources, targets, sems):
     copies = [pltpu.make_async_copy(a, b, sems.at[n])
               for n, (a, b) in enumerate(zip(sources, targets))]
-    for copy in copies:
-        copy.start()
+    for n in (2, 3, 0, 1, 4, 5, 6):
+        copies[n].start()
     return copies
 
 
@@ -103,14 +118,18 @@
     copies = fetch_all(sources, targets, sems)
     d_ref, m_ref, _, plane_ref, h_ref = targets[:5]
     size_x, size_y, size_z = d_ref.shape
-    for copy in copies[:4]:
-        copy.wait()
+    across = (((1,), (1,)), ((), ()))
+    copies[2].wait()
+    copies[3].wait()
+    line = stacked_rows(line_ref[...])
+    plane = stacked_columns(four_quadrants(plane_ref[...]))
+    copies[0].wait()
+    copies[1].wait()
     flat = (m_ref[...] / d_ref[...]).reshape(size_x * size_y, size_z)
-    across = (((1,), (1,)), ((), ()))
-    along = lax.dot_general(line_ref[...], flat, across, precision=HIGHEST,
-                            preferred_element_type=jnp.float32)
-    both = lax.dot_general(along, four_quadrants(plane_ref[...]), across, precision=HIGHEST,
-                           preferred_element_type=jnp.float32)
+    along = fold(lax.dot_general(line, stacked_columns(flat), across,
+                                 preferred_element_type=jnp.float32))
+    both = fold(lax.dot_general(stacked_rows(along), plane, across,
+                                preferred_element_type=jnp.float32))
     part = jnp.where(lanes_of((4, 128)) < 64, both[0:4], both[4:8])
     part_ref[...] = jnp.broadcast_to(part[None], (slots, 4, 128))
     send = pltpu.make_async_copy(part_ref, part_out, part_sem)
@@ -152,8 +171,8 @@
     return counts[0:4]
 
 
-def local_kernel(d_ref, m_ref, h_ref, modes_ref, density_ref, momentum_ref, hydrogen_ref,
-                 weight_ref, pad_ref):
+def local_kernel(d_ref, m_ref, h_ref, modes_ref, plane_ref, density_ref, momentum_ref,
+                 hydrogen_ref, weight_ref, plane_out, pad_ref):
     size_x, size_y, size_z = d_ref.shape
     dens = [d_ref[i] for i in range(size_x)]
     mom = [m_ref[i] for i in range(size_x)]
@@ -198,6 +217,8 @@
         hydrogen_ref[i] = (DIFFUSIVITY * second_diffs(1, fuel, i) - first_diff(carried, i)
                            - fuel[i] * jnp.exp(-ACTIVATION * fuel[i] / dens[i]))
     weight_ref[...] = mode_counts(modes_ref[...])
+    plane_out[...] = jnp.concatenate(
+        split(four_quadrants(plane_ref[...])), 0).astype(jnp.bfloat16)
 
 
 def edge_kernel(density_part, momentum_part, hydrogen_part, before_ref, after_ref, side_prev_ref,
@@ -286,8 +307,7 @@
     other = swap64(coef)
     spec = jnp.where(quad == 3, -coef, coef) + jnp.where(quad == 2, -other, other)
     spec = jnp.concatenate([jnp.where(quad < 2, spec, 0.0), jnp.where(quad < 2, 0.0, spec)], 0)
-    mid = jnp.dot(spec, four_quadrants(plane_ref[...]), precision=HIGHEST,
-                  preferred_element_type=jnp.float32)
+    mid = fold(jnp.dot(stacked_rows(spec), plane_ref[...], preferred_element_type=jnp.float32))
     high, middle, rest = split(mid)
     mid = jnp.concatenate([high, high, high, middle, middle, rest], 0).astype(jnp.bfloat16)
     low = lax.dot_general(mid, line_ref[...], (((0,), (0,)), ((), ())),
@@ -360,12 +380,13 @@
     pad = pltpu.VMEM((2, size_x, 16 + size_y, size_z), f32)
     own = pl.pallas_call(
         local_kernel,
-        in_specs=[VMEM_SPEC] * 4,
-        out_specs=[VMEM_SPEC] * 4,
-        out_shape=[block_vmem] * 3 + [pltpu.VMEM((4, 128), f32)],
+        in_specs=[VMEM_SPEC] * 5,
+        out_specs=[VMEM_SPEC] * 5,
+        out_shape=[block_vmem] * 3 + [pltpu.VMEM((4, 128), f32),
+                                      pltpu.VMEM((384, size_x * size_y), jnp.bfloat16)],
         scratch_shapes=[pad],
-    )(*in_vmem(density, momentum, hydrogen, modes))
-    weight = own[3]
+    )(*in_vmem(density, momentum, hydrogen, modes, plane))
+    weight, plane = own[3:]
     rates = pl.pallas_call(
         edge_kernel,
         in_specs=[VMEM_SPEC] * 7,

time: 20.6 us -> 20.3 us (0.985)
  Pallas kernels: 3.91 us -> 3.58 us
    pallas_call x1, Pallas kernels: 2.2 us -> 1.92 us  [per_device(): pl.pallas_call(functools.partial(pre_kernel, slots), in_specs=[ANY_SPEC]...]
  transfers between devices with their start and end apart: 6 -> 6, of which waited for: 1 -> 1; matrix products, arithmetic and copies ran while one was open for 0% -> 0% of each run, Pallas kernels for 2% -> 3%
where the time goes in v2:
time: 20.3 us; the launch traced here: 20.1 us
  starting transfers between devices  14.7 us (72%)
  Pallas kernels  3.58 us (18%)
  waiting for transfers between devices  1.09 us (5%)
  between operations  0.68 us (3%)
    ppermute x5, starting transfers between devices, shift(): return lax.ppermute(x, axis, [(i, (i + step) % size) for i in range(size)])  7.39 us
    all_to_all x1, starting transfers between devices, per_device(): parts = lax.all_to_all(parts, AXES, 0, 0)  7.33 us
    pallas_call x1, Pallas kernels, per_device(): pl.pallas_call(functools.partial(pre_kernel, slots), in_specs=[ANY_SPEC]...  1.92 us
    pallas_call x1, Pallas kernels, per_device(): pl.pallas_call(functools.partial(post_kernel, float(math.prod(full))), in...  1.15 us
    ppermute x5, waiting for transfers between devices, shift(): return lax.ppermute(x, axis, [(i, (i + step) % size) for i in range(size)])  1.09 us
  transfers between devices with their start and end apart: 6, of which 1 were waited for; matrix products, arithmetic and copies ran while one was open for 0% of the time, Pallas kernels for 3%

profile of v2, /device:TPU:0, one launch (start us, length us, event | category | flops | bytes accessed | tf_op | source)
XLA Modules:
  0.0 20.1 jit_solution(1127534401835514757)
XLA Ops:
  0.6 1.9 %shard_map.85 = (f32[8,16,128]{2,1,0:T(8,128)S(1)}, f32[8,16,128]{2,1,0:T(8,128)S(1)}, f32[64,128]{1,0:T(8,128)S(1)}, f32[8,16,128]{2,1,0:T(8,128)S(1)}, bf16[48...) custom-call(f32[8,16,128]{2,1,0:T(8,128)} %refs_0_.1, ...), custom_call_target="tpu_custom_call" | custom-call | tf_op jit(solution)/shard_map/pallas_call | solution.py:357
  2.6 7.3 %all-to-all-start = ((f32[32,4,128]{2,1,0:T(4,128)}), f32[32,4,128]{2,1,0:T(4,128)S(1)}, u32[]{:S(2)}, u32[]{:S(2)}) async-start(f32[32,4,128]{2,1,0:T(4,128)} %get-tuple-element.37), calls=%async_computation | async-start | bytes 131072 | tf_op jit(solution)/shard_map/all_to_all | solution.py:371
  9.9 0.3 %collective-permute-start = (f32[3,4,16,128]{3,2,1,0:T(8,128)S(1)}, f32[3,4,16,128]{3,2,1,0:T(8,128)S(1)}, u32[]{:S(2)}, u32[]{:S(2)}) collective-permute-start(f32[3,4,16,128]{3,2,1,0:T(8,128)S(1)} %get-tuple-element.30), channel_id=1, source_target_pairs={{0,8},{8,16},{16,24},{24,0},{1,9},{9,17},{17,25},{25,1},{2,10},{10... | collective-permute-start | bytes 294920 | tf_op jit(solution)/shard_map/ppermute | solution.py:337
  10.2 1.5 %collective-permute-start.1 = (f32[3,4,16,128]{3,2,1,0:T(8,128)S(1)}, f32[3,4,16,128]{3,2,1,0:T(8,128)S(1)}, u32[]{:S(2)}, u32[]{:S(2)}) collective-permute-start(f32[3,4,16,128]{3,2,1,0:T(8,128)S(1)} %get-tuple-element.31), channel_id=1, source_target_pairs={{0,24},{8,0},{16,8},{24,16},{1,25},{9,1},{17,9},{25,17},{2,26},{10... | collective-permute-start | bytes 294920 | tf_op jit(solution)/shard_map/ppermute | solution.py:337
  11.7 1.8 %collective-permute-start.2 = (f32[2,8,8,128]{3,2,1,0:T(8,128)S(1)}, f32[2,8,8,128]{3,2,1,0:T(8,128)S(1)}, u32[]{:S(2)}, u32[]{:S(2)}) collective-permute-start(f32[2,8,8,128]{3,2,1,0:T(8,128)S(1)} %get-tuple-element.32), channel_id=1, source_target_pairs={{0,4},{4,0},{1,5},{5,1},{2,6},{6,2},{3,7},{7,3},{8,12},{12,8},{9,1... | collective-permute-start | bytes 196616 | tf_op jit(solution)/shard_map/ppermute | solution.py:337
  13.5 1.5 %collective-permute-start.3 = (f32[16,128]{1,0:T(8,128)S(1)}, f32[16,128]{1,0:T(8,128)S(1)}, u32[]{:S(2)}, u32[]{:S(2)}) collective-permute-start(f32[16,128]{1,0:T(8,128)S(1)} %get-tuple-element.36), channel_id=1, source_target_pairs={{0,1},{1,2},{2,3},{3,0},{4,5},{5,6},{6,7},{7,4},{8,9},{9,10},{10,1... | collective-permute-start | bytes 24584 | tf_op jit(solution)/shard_map/ppermute | solution.py:337
  14.9 2.4 %collective-permute-start.4 = (f32[16,128]{1,0:T(8,128)S(1)}, f32[16,128]{1,0:T(8,128)S(1)}, u32[]{:S(2)}, u32[]{:S(2)}) collective-permute-start(f32[16,128]{1,0:T(8,128)S(1)} %get-tuple-element.36), channel_id=1, source_target_pairs={{0,3},{1,0},{2,1},{3,2},{4,7},{5,4},{6,5},{7,6},{8,11},{9,8},{10,9... | collective-permute-start | bytes 24584 | tf_op jit(solution)/shard_map/ppermute | solution.py:337
  17.3 0.4 %shard_map.86 = (f32[8,16,128]{2,1,0:T(8,128)S(1)}, f32[8,16,128]{2,1,0:T(8,128)S(1)}, f32[8,16,128]{2,1,0:T(8,128)S(1)}, f32[4,128]{1,0:T(4,128)S(1)}, bf16[384,128]{1,0:T(8,128)(2,1)S(1)}) custom-call(f32[8,16,128]{2,1,0:T(8,128)S(1)} %get-tuple-element.22.d_ref, f32[8,16,128]{2,1,0:T(8,128)S(1)} %get-tuple-element.23.m_ref, ...), custom_call_target="tpu_custom_call" | custom-call | tf_op jit(solution)/shard_map/pallas_call | solution.py:381
  17.6 0.0 collective-permute-done.2.side_prev_ref.side_next_ref
  17.7 0.0 collective-permute-done.before_ref
  17.7 0.0 collective-permute-done.1.after_ref
  17.7 0.2 shard_map.87
  17.8 1.1 %collective-permute-done.3.depth_prev_ref = f32[16,128]{1,0:T(8,128)S(1)} collective-permute-done((f32[16,128]{1,0:T(8,128)S(1)}, f32[16,128]{1,0:T(8,128)S(1)}, u32[]{:S(2)}, u32[]{:S(2)}) %collective-permute-start.3) | collective-permute-done | bytes 8224 | tf_op jit(solution)/shard_map/ppermute | solution.py:337
  18.9 0.0 collective-permute-done.4.depth_next_ref
  18.9 0.0 all-to-all-done.parts_ref
  18.9 1.2 %shard_map.88 = (f32[8,16,128]{2,1,0:T(8,128)}, f32[8,16,128]{2,1,0:T(8,128)}, f32[8,16,128]{2,1,0:T(8,128)}) custom-call(f32[8,16,128]{2,1,0:T(8,128)S(1)} %get-tuple-element.22.d_ref, f32[8,16,128]{2,1,0:T(8,128)S(1)} %get-tuple-element.33.density_ref, f32[8,16,128]{2,1,0:T(8,128)S(1)} %get-tuple-element.34.momentum_ref, ...), custom_call_target="tpu_custom_call" | custom-call | tf_op jit(solution)/shard_map/pallas_call | solution.py:397
Async XLA Ops:
  2.6 16.4 %all-to-all-start = ((f32[32,4,128]{2,1,0:T(4,128)}), f32[32,4,128]{2,1,0:T(4,128)S(1)}, u32[]{:S(2)}, u32[]{:S(2)}) async-start(f32[32,4,128]{2,1,0:T(4,128)} %get-tuple-element.37), calls=%async_computation | async-start | bytes 131072 | tf_op jit(solution)/shard_map/all_to_all | solution.py:371
  9.9 7.8 %collective-permute-start = (f32[3,4,16,128]{3,2,1,0:T(8,128)S(1)}, f32[3,4,16,128]{3,2,1,0:T(8,128)S(1)}, u32[]{:S(2)}, u32[]{:S(2)}) collective-permute-start(f32[3,4,16,128]{3,2,1,0:T(8,128)S(1)} %get-tuple-element.30), channel_id=1, source_target_pairs={{0,8},{8,16},{16,24},{24,0},{1,9},{9,17},{17,25},{25,1},{2,10},{10... | collective-permute-start | bytes 294920 | tf_op jit(solution)/shard_map/ppermute | solution.py:337
  10.2 7.5 %collective-permute-start.1 = (f32[3,4,16,128]{3,2,1,0:T(8,128)S(1)}, f32[3,4,16,128]{3,2,1,0:T(8,128)S(1)}, u32[]{:S(2)}, u32[]{:S(2)}) collective-permute-start(f32[3,4,16,128]{3,2,1,0:T(8,128)S(1)} %get-tuple-element.31), channel_id=1, source_target_pairs={{0,24},{8,0},{16,8},{24,16},{1,25},{9,1},{17,9},{25,17},{2,26},{10... | collective-permute-start | bytes 294920 | tf_op jit(solution)/shard_map/ppermute | solution.py:337
  11.7 6.0 %collective-permute-start.2 = (f32[2,8,8,128]{3,2,1,0:T(8,128)S(1)}, f32[2,8,8,128]{3,2,1,0:T(8,128)S(1)}, u32[]{:S(2)}, u32[]{:S(2)}) collective-permute-start(f32[2,8,8,128]{3,2,1,0:T(8,128)S(1)} %get-tuple-element.32), channel_id=1, source_target_pairs={{0,4},{4,0},{1,5},{5,1},{2,6},{6,2},{3,7},{7,3},{8,12},{12,8},{9,1... | collective-permute-start | bytes 196616 | tf_op jit(solution)/shard_map/ppermute | solution.py:337
  13.5 5.4 %collective-permute-start.3 = (f32[16,128]{1,0:T(8,128)S(1)}, f32[16,128]{1,0:T(8,128)S(1)}, u32[]{:S(2)}, u32[]{:S(2)}) collective-permute-start(f32[16,128]{1,0:T(8,128)S(1)} %get-tuple-element.36), channel_id=1, source_target_pairs={{0,1},{1,2},{2,3},{3,0},{4,5},{5,6},{6,7},{7,4},{8,9},{9,10},{10,1... | collective-permute-start | bytes 24584 | tf_op jit(solution)/shard_map/ppermute | solution.py:337
  14.9 4.0 %collective-permute-start.4 = (f32[16,128]{1,0:T(8,128)S(1)}, f32[16,128]{1,0:T(8,128)S(1)}, u32[]{:S(2)}, u32[]{:S(2)}) collective-permute-start(f32[16,128]{1,0:T(8,128)S(1)} %get-tuple-element.36), channel_id=1, source_target_pairs={{0,3},{1,0},{2,1},{3,2},{4,7},{5,4},{6,5},{7,6},{8,11},{9,8},{10,9... | collective-permute-start | bytes 24584 | tf_op jit(solution)/shard_map/ppermute | solution.py:337

commit v3 on v2

--- a/solution.py
+++ b/solution.py
@@ -102,7 +102,7 @@
 def fetch_all(sources, targets, sems):
     copies = [pltpu.make_async_copy(a, b, sems.at[n])
               for n, (a, b) in enumerate(zip(sources, targets))]
-    for n in (2, 3, 0, 1, 4, 5, 6):
+    for n in (0, 1, 2, 3, 4, 5, 6):
         copies[n].start()
     return copies
 
@@ -303,7 +303,7 @@
     other = swap64(total)
     waves = jnp.where(quad == 3, -total, total) + jnp.where(quad == 0, -other, other)
     coef = weight_ref[...] * waves
-    energy = jnp.sum(coef * waves)
+    energy = jnp.sum(jnp.sum(coef * waves, axis=1, keepdims=True), axis=0, keepdims=True)
     other = swap64(coef)
     spec = jnp.where(quad == 3, -coef, coef) + jnp.where(quad == 2, -other, other)
     spec = jnp.concatenate([jnp.where(quad < 2, spec, 0.0), jnp.where(quad < 2, 0.0, spec)], 0)
@@ -313,7 +313,7 @@
     low = lax.dot_general(mid, line_ref[...], (((0,), (0,)), ((), ())),
                           preferred_element_type=jnp.float32)
     scale = 2.0 * FORCE_POWER / (energy + ENERGY_EPS)
-    force = low.reshape(size_x, size_y, size_z) * scale
+    force = (low * scale).reshape(size_x, size_y, size_z)
     for i in range(size_x):
         part = momentum_ref[i] + VISCOSITY * depth_part(0, i)
         buffer_ref[1, i] = part + d_ref[i] * force[i]

time: 20.3 us -> 20.2 us (level)
  no operation moved by 1% of the time
where the time goes in v3:
time: 20.2 us; the launch traced here: 20 us
  starting transfers between devices  14.7 us (73%)
  Pallas kernels  3.54 us (18%)
  waiting for transfers between devices  1.09 us (5%)
  between operations  0.68 us (3%)
    ppermute x5, starting transfers between devices, shift(): return lax.ppermute(x, axis, [(i, (i + step) % size) for i in range(size)])  7.39 us
    all_to_all x1, starting transfers between devices, per_device(): parts = lax.all_to_all(parts, AXES, 0, 0)  7.33 us
    pallas_call x1, Pallas kernels, per_device(): pl.pallas_call(functools.partial(pre_kernel, slots), in_specs=[ANY_SPEC]...  1.88 us
    pallas_call x1, Pallas kernels, per_device(): pl.pallas_call(functools.partial(post_kernel, float(math.prod(full))), in...  1.16 us
    ppermute x5, waiting for transfers between devices, shift(): return lax.ppermute(x, axis, [(i, (i + step) % size) for i in range(size)])  1.09 us
  transfers between devices with their start and end apart: 6, of which 1 were waited for; matrix products, arithmetic and copies ran while one was open for 0% of the time, Pallas kernels for 3%

profile of v3, /device:TPU:0, one launch (start us, length us, event | category | flops | bytes accessed | tf_op | source)
XLA Modules:
  0.0 20.0 jit_solution(361261047799823674)
XLA Ops:
  0.6 1.9 %shard_map.85 = (f32[8,16,128]{2,1,0:T(8,128)S(1)}, f32[8,16,128]{2,1,0:T(8,128)S(1)}, f32[64,128]{1,0:T(8,128)S(1)}, f32[8,16,128]{2,1,0:T(8,128)S(1)}, bf16[48...) custom-call(f32[8,16,128]{2,1,0:T(8,128)} %refs_0_.1, ...), custom_call_target="tpu_custom_call" | custom-call | tf_op jit(solution)/shard_map/pallas_call | solution.py:357
  2.5 7.3 %all-to-all-start = ((f32[32,4,128]{2,1,0:T(4,128)}), f32[32,4,128]{2,1,0:T(4,128)S(1)}, u32[]{:S(2)}, u32[]{:S(2)}) async-start(f32[32,4,128]{2,1,0:T(4,128)} %get-tuple-element.37), calls=%async_computation | async-start | bytes 131072 | tf_op jit(solution)/shard_map/all_to_all | solution.py:371
  9.9 0.3 %collective-permute-start = (f32[3,4,16,128]{3,2,1,0:T(8,128)S(1)}, f32[3,4,16,128]{3,2,1,0:T(8,128)S(1)}, u32[]{:S(2)}, u32[]{:S(2)}) collective-permute-start(f32[3,4,16,128]{3,2,1,0:T(8,128)S(1)} %get-tuple-element.30), channel_id=1, source_target_pairs={{0,8},{8,16},{16,24},{24,0},{1,9},{9,17},{17,25},{25,1},{2,10},{10... | collective-permute-start | bytes 294920 | tf_op jit(solution)/shard_map/ppermute | solution.py:337
  10.2 1.5 %collective-permute-start.1 = (f32[3,4,16,128]{3,2,1,0:T(8,128)S(1)}, f32[3,4,16,128]{3,2,1,0:T(8,128)S(1)}, u32[]{:S(2)}, u32[]{:S(2)}) collective-permute-start(f32[3,4,16,128]{3,2,1,0:T(8,128)S(1)} %get-tuple-element.31), channel_id=1, source_target_pairs={{0,24},{8,0},{16,8},{24,16},{1,25},{9,1},{17,9},{25,17},{2,26},{10... | collective-permute-start | bytes 294920 | tf_op jit(solution)/shard_map/ppermute | solution.py:337
  11.7 1.8 %collective-permute-start.2 = (f32[2,8,8,128]{3,2,1,0:T(8,128)S(1)}, f32[2,8,8,128]{3,2,1,0:T(8,128)S(1)}, u32[]{:S(2)}, u32[]{:S(2)}) collective-permute-start(f32[2,8,8,128]{3,2,1,0:T(8,128)S(1)} %get-tuple-element.32), channel_id=1, source_target_pairs={{0,4},{4,0},{1,5},{5,1},{2,6},{6,2},{3,7},{7,3},{8,12},{12,8},{9,1... | collective-permute-start | bytes 196616 | tf_op jit(solution)/shard_map/ppermute | solution.py:337
  13.4 1.5 %collective-permute-start.3 = (f32[16,128]{1,0:T(8,128)S(1)}, f32[16,128]{1,0:T(8,128)S(1)}, u32[]{:S(2)}, u32[]{:S(2)}) collective-permute-start(f32[16,128]{1,0:T(8,128)S(1)} %get-tuple-element.36), channel_id=1, source_target_pairs={{0,1},{1,2},{2,3},{3,0},{4,5},{5,6},{6,7},{7,4},{8,9},{9,10},{10,1... | collective-permute-start | bytes 24584 | tf_op jit(solution)/shard_map/ppermute | solution.py:337
  14.9 2.4 %collective-permute-start.4 = (f32[16,128]{1,0:T(8,128)S(1)}, f32[16,128]{1,0:T(8,128)S(1)}, u32[]{:S(2)}, u32[]{:S(2)}) collective-permute-start(f32[16,128]{1,0:T(8,128)S(1)} %get-tuple-element.36), channel_id=1, source_target_pairs={{0,3},{1,0},{2,1},{3,2},{4,7},{5,4},{6,5},{7,6},{8,11},{9,8},{10,9... | collective-permute-start | bytes 24584 | tf_op jit(solution)/shard_map/ppermute | solution.py:337
  17.2 0.4 %shard_map.86 = (f32[8,16,128]{2,1,0:T(8,128)S(1)}, f32[8,16,128]{2,1,0:T(8,128)S(1)}, f32[8,16,128]{2,1,0:T(8,128)S(1)}, f32[4,128]{1,0:T(4,128)S(1)}, bf16[384,128]{1,0:T(8,128)(2,1)S(1)}) custom-call(f32[8,16,128]{2,1,0:T(8,128)S(1)} %get-tuple-element.22.d_ref, f32[8,16,128]{2,1,0:T(8,128)S(1)} %get-tuple-element.23.m_ref, ...), custom_call_target="tpu_custom_call" | custom-call | tf_op jit(solution)/shard_map/pallas_call | solution.py:381
  17.6 0.0 collective-permute-done.2.side_prev_ref.side_next_ref
  17.6 0.0 collective-permute-done.before_ref
  17.6 0.0 collective-permute-done.1.after_ref
  17.6 0.2 shard_map.87
  17.8 1.1 %collective-permute-done.3.depth_prev_ref = f32[16,128]{1,0:T(8,128)S(1)} collective-permute-done((f32[16,128]{1,0:T(8,128)S(1)}, f32[16,128]{1,0:T(8,128)S(1)}, u32[]{:S(2)}, u32[]{:S(2)}) %collective-permute-start.3) | collective-permute-done | bytes 8224 | tf_op jit(solution)/shard_map/ppermute | solution.py:337
  18.9 0.0 collective-permute-done.4.depth_next_ref
  18.9 0.0 all-to-all-done.parts_ref
  18.9 1.2 %shard_map.88 = (f32[8,16,128]{2,1,0:T(8,128)}, f32[8,16,128]{2,1,0:T(8,128)}, f32[8,16,128]{2,1,0:T(8,128)}) custom-call(f32[8,16,128]{2,1,0:T(8,128)S(1)} %get-tuple-element.22.d_ref, f32[8,16,128]{2,1,0:T(8,128)S(1)} %get-tuple-element.33.density_ref, f32[8,16,128]{2,1,0:T(8,128)S(1)} %get-tuple-element.34.momentum_ref, ...), custom_call_target="tpu_custom_call" | custom-call | tf_op jit(solution)/shard_map/pallas_call | solution.py:397
Async XLA Ops:
  2.5 16.4 %all-to-all-start = ((f32[32,4,128]{2,1,0:T(4,128)}), f32[32,4,128]{2,1,0:T(4,128)S(1)}, u32[]{:S(2)}, u32[]{:S(2)}) async-start(f32[32,4,128]{2,1,0:T(4,128)} %get-tuple-element.37), calls=%async_computation | async-start | bytes 131072 | tf_op jit(solution)/shard_map/all_to_all | solution.py:371
  9.9 7.8 %collective-permute-start = (f32[3,4,16,128]{3,2,1,0:T(8,128)S(1)}, f32[3,4,16,128]{3,2,1,0:T(8,128)S(1)}, u32[]{:S(2)}, u32[]{:S(2)}) collective-permute-start(f32[3,4,16,128]{3,2,1,0:T(8,128)S(1)} %get-tuple-element.30), channel_id=1, source_target_pairs={{0,8},{8,16},{16,24},{24,0},{1,9},{9,17},{17,25},{25,1},{2,10},{10... | collective-permute-start | bytes 294920 | tf_op jit(solution)/shard_map/ppermute | solution.py:337
  10.2 7.5 %collective-permute-start.1 = (f32[3,4,16,128]{3,2,1,0:T(8,128)S(1)}, f32[3,4,16,128]{3,2,1,0:T(8,128)S(1)}, u32[]{:S(2)}, u32[]{:S(2)}) collective-permute-start(f32[3,4,16,128]{3,2,1,0:T(8,128)S(1)} %get-tuple-element.31), channel_id=1, source_target_pairs={{0,24},{8,0},{16,8},{24,16},{1,25},{9,1},{17,9},{25,17},{2,26},{10... | collective-permute-start | bytes 294920 | tf_op jit(solution)/shard_map/ppermute | solution.py:337
  11.7 6.0 %collective-permute-start.2 = (f32[2,8,8,128]{3,2,1,0:T(8,128)S(1)}, f32[2,8,8,128]{3,2,1,0:T(8,128)S(1)}, u32[]{:S(2)}, u32[]{:S(2)}) collective-permute-start(f32[2,8,8,128]{3,2,1,0:T(8,128)S(1)} %get-tuple-element.32), channel_id=1, source_target_pairs={{0,4},{4,0},{1,5},{5,1},{2,6},{6,2},{3,7},{7,3},{8,12},{12,8},{9,1... | collective-permute-start | bytes 196616 | tf_op jit(solution)/shard_map/ppermute | solution.py:337
  13.4 5.4 %collective-permute-start.3 = (f32[16,128]{1,0:T(8,128)S(1)}, f32[16,128]{1,0:T(8,128)S(1)}, u32[]{:S(2)}, u32[]{:S(2)}) collective-permute-start(f32[16,128]{1,0:T(8,128)S(1)} %get-tuple-element.36), channel_id=1, source_target_pairs={{0,1},{1,2},{2,3},{3,0},{4,5},{5,6},{6,7},{7,4},{8,9},{9,10},{10,1... | collective-permute-start | bytes 24584 | tf_op jit(solution)/shard_map/ppermute | solution.py:337
  14.9 4.0 %collective-permute-start.4 = (f32[16,128]{1,0:T(8,128)S(1)}, f32[16,128]{1,0:T(8,128)S(1)}, u32[]{:S(2)}, u32[]{:S(2)}) collective-permute-start(f32[16,128]{1,0:T(8,128)S(1)} %get-tuple-element.36), channel_id=1, source_target_pairs={{0,3},{1,0},{2,1},{3,2},{4,7},{5,4},{6,5},{7,6},{8,11},{9,8},{10,9... | collective-permute-start | bytes 24584 | tf_op jit(solution)/shard_map/ppermute | solution.py:337
